TPU v7x, 32 devices: a whole 2x2x4 slice. The times are simulated.
32 devices in a mesh: dp: 4 (over z), ctx: 4 (over y, core), tp: 2 (over x).
Axes of the slice: x: 2, y: 2, z: 4, core: 2. Of those that a mesh axis runs over, the one named last changes fastest.
Arguments:
- hidden: bfloat16 [4, 512, 4096], P('dp', 'ctx'), may hold values from -6 to 6
- query_heads: bfloat16 [4, 512, 4096], P('dp', 'ctx', 'tp'), may hold values from -6 to 6
- key_heads: bfloat16 [4, 512, 512], P('dp', 'ctx', 'tp'), may hold values from -6 to 6
- value_heads: bfloat16 [4, 512, 512], P('dp', 'ctx', 'tp'), may hold values from -6 to 6
- attention_out: bfloat16 [4, 512, 4096], P('dp', 'ctx', 'tp'), may hold values from -3 to 3
- output_grad: bfloat16 [4, 512, 4096], P('dp', 'ctx', 'tp'), may hold values from -3 to 3
- log_norm: float32 [4, 32, 512], P('dp', 'tp', 'ctx'), may hold values from -40 to 40, as said below
- block_order: int32 [8], replicated, may hold values from 0 to 7, as said below
- value_weight: bfloat16 [4096, 512], P(None, 'tp'), may hold values from -0.25 to 0.25
Outputs:
- query_grad: bfloat16 [4, 512, 4096], P('dp', 'ctx', 'tp')
- key_grad: bfloat16 [4, 512, 512], P('dp', 'ctx', 'tp')
- value_grad: bfloat16 [4, 512, 512], P('dp', 'ctx', 'tp')
- hidden_grad: bfloat16 [4, 512, 4096], P('dp', 'ctx', 'tp')
- weight_grad: float32 [4096, 512], P('ctx', 'tp')
Inputs may be any that keep to these rules, and one draw needn't show every extreme that they name: `block_order`: each of 0 to 7 once. log_norm is the log of the sum of exp(scores) over the keys visible to that row, so the probabilities of each row and head sum to one.
All inputs are finite; a program needn't handle non-finite values.
Results may differ from a plain program's by a relative error of at most 0.025.
Values may be sent and summed in bfloat16 or wider, within the bound.
No kernel may reach another device: no remote copies, remote signals or barrier semaphores. Data moves between devices by JAX's collectives and lax.ppermute only.
A program may use at most 64 MiB of HBM per device.

v0:
```python
import jax
import jax.numpy as jnp
from jax import lax
from jax.experimental import pallas as pl
from jax.experimental.pallas import tpu as pltpu
from jax.sharding import PartitionSpec as P


HD = 128
HQ = 32
KVH = 4
F32 = jnp.float32
BF16 = jnp.bfloat16
NT = (((1,), (1,)), ((), ()))
NN = (((1,), (0,)), ((), ()))


def is_pow2(n):
    return n & (n - 1) == 0


def after(x, *deps):
    return lax.optimization_barrier((x, deps))[0]


def swap(x, axis, s):
    n = lax.axis_size(axis)
    return lax.ppermute(x, axis, [(i, i ^ s) for i in range(n)])


def probability(meta, q_pair, norm_pair, key_ref, s, tokens):
    rank = meta[0]
    block = tokens // 2
    lane = lax.broadcasted_iota(jnp.int32, (1, 2 * tokens), 1) % tokens
    q_first = jnp.where(lane < block, meta[1 + 2 * rank], meta[2 + 2 * rank])
    q_pos = q_first * block + lane % block
    owner = rank ^ s
    row = lax.broadcasted_iota(jnp.int32, (tokens, 1), 0)
    k_first = jnp.where(row < block, meta[1 + 2 * owner], meta[2 + 2 * owner])
    k_pos = k_first * block + row % block
    scores = lax.dot_general(key_ref[0], q_pair, NT, preferred_element_type=F32)
    shifted = scores * (HD ** (-0.5)) - norm_pair
    return jnp.exp(jnp.where(k_pos <= q_pos, shifted, -jnp.inf))


def pair_of(ref, h):
    return jnp.concatenate(
        [ref[0, :, h * HD : (h + 1) * HD], ref[0, :, (h + 1) * HD : (h + 2) * HD]], axis=0
    )


def rows_of(ref, h):
    return jnp.concatenate([ref[0, h : h + 1, :], ref[0, h + 1 : h + 2, :]], axis=1)


def value_kernel(n, members, tokens, meta, q_ref, g_ref, norm_ref, *rest):
    keys, out_ref, weights = rest[:n], rest[n], rest[n + 1]
    g_all = jnp.concatenate([g_ref[0, :, h * HD : (h + 1) * HD] for h in range(members)], axis=0)
    for h in range(0, members, 2):
        q_pair = pair_of(q_ref, h)
        norm_pair = rows_of(norm_ref, h)
        for s in range(n):
            p = probability(meta, q_pair, norm_pair, keys[s], s, tokens)
            weights[s * tokens : (s + 1) * tokens, h * tokens : (h + 2) * tokens] = p.astype(BF16)
    grad = lax.dot_general(weights[...], g_all, NN, preferred_element_type=F32).astype(BF16)
    for s in range(n):
        out_ref[meta[0] ^ s] = grad[s * tokens : (s + 1) * tokens]


def turn_kernel(n, tokens, meta, *refs):
    for s in range(n):
        start = pl.multiple_of((meta[0] ^ s) * tokens, tokens)
        refs[n][:, pl.ds(start, tokens)] = refs[s][...].T


def weight_kernel(n, half, tokens, meta, mine_ref, got_ref, turned, first_ref, second_ref, own_ref):
    rows = (mine_ref[...].astype(F32) + got_ref[...].astype(F32)).astype(BF16)
    owner = meta[0]
    own_ref[...] = (mine_ref[owner].astype(F32) + got_ref[owner].astype(F32)).astype(BF16)
    rows = rows.reshape(n * tokens, HD)
    first_ref[...] = lax.dot_general(
        turned[:half], rows, NN, preferred_element_type=F32
    ).astype(BF16)
    second_ref[...] = lax.dot_general(
        turned[half:], rows, NN, preferred_element_type=F32
    ).astype(BF16)


def slope_kernel(n, members, tokens, meta, q_ref, g_ref, o_ref, norm_ref, *rest):
    keys, values = rest[:n], rest[n : 2 * n]
    dq_ref, dk_ref, slopes, deltas = rest[2 * n :]
    q_all = jnp.concatenate([q_ref[0, :, h * HD : (h + 1) * HD] for h in range(members)], axis=0)
    for h in range(members):
        prod = (
            g_ref[0, :, h * HD : (h + 1) * HD].astype(F32)
            * o_ref[0, :, h * HD : (h + 1) * HD].astype(F32)
        )
        deltas[0, h : h + 1, :] = jnp.sum(prod.T, axis=0, keepdims=True)
    for h in range(0, members, 2):
        q_pair = pair_of(q_ref, h)
        g_pair = pair_of(g_ref, h)
        norm_pair = rows_of(norm_ref, h)
        delta_pair = rows_of(deltas, h)
        for s in range(n):
            p = probability(meta, q_pair, norm_pair, keys[s], s, tokens)
            through = lax.dot_general(values[s][0], g_pair, NT, preferred_element_type=F32)
            slopes[s * tokens : (s + 1) * tokens, h * tokens : (h + 2) * tokens] = (
                p * (through - delta_pair)
            ).astype(BF16)
    grad = lax.dot_general(slopes[...], q_all, NN, preferred_element_type=F32).astype(BF16)
    for s in range(n):
        dk_ref[s] = grad[s * tokens : (s + 1) * tokens]
    keys_t = jnp.concatenate([keys[s][0] for s in range(n)], axis=0).T
    dq_t = lax.dot_general(keys_t, slopes[...], NN, preferred_element_type=F32) * (HD ** (-0.5))
    for h in range(members):
        dq_ref[0, :, h * HD : (h + 1) * HD] = dq_t[:, h * tokens : (h + 1) * tokens].T.astype(BF16)


def shards(
    hidden,
    query_heads,
    key_heads,
    value_heads,
    attention_out,
    output_grad,
    log_norm,
    block_order,
    value_weight,
):
    tokens = query_heads.shape[1]
    groups = key_heads.shape[2] // HD
    members = HQ // KVH
    n = lax.axis_size("ctx")
    dp = lax.axis_size("dp")
    tp = lax.axis_size("tp")
    rank = lax.axis_index("ctx")
    wide = members * HD
    meta = jnp.concatenate([rank[None].astype(jnp.int32), block_order])

    keys = [key_heads] + [swap(key_heads, "ctx", s) for s in range(1, n)]
    values = [value_heads] + [swap(value_heads, "ctx", s) for s in range(1, n)]

    smem = pl.BlockSpec(memory_space=pltpu.SMEM)

    def value_terms(g):
        col = lambda i: (0, 0, g)
        return pl.pallas_call(
            lambda *refs: value_kernel(n, members, tokens, *refs),
            grid=(1,),
            in_specs=[
                smem,
                pl.BlockSpec((1, tokens, wide), col),
                pl.BlockSpec((1, tokens, wide), col),
                pl.BlockSpec((1, members, tokens), lambda i: (0, g, 0)),
            ]
            + [pl.BlockSpec((1, tokens, HD), col)] * n,
            out_specs=pl.BlockSpec((n, tokens, HD), lambda i: (0, 0, 0)),
            out_shape=jax.ShapeDtypeStruct((n, tokens, HD), BF16),
            scratch_shapes=[pltpu.VMEM((n * tokens, members * tokens), BF16)],
        )(meta, query_heads, output_grad, log_norm, *keys)

    width = hidden.shape[2] // n
    split_dp = dp > 1 and is_pow2(dp) and width % dp == 0 and dp <= 4
    half = width // 2
    dp_rank = lax.axis_index("dp")
    low = dp_rank % 2
    held = hidden[0]

    def columns(owner):
        start = owner * width
        if not split_dp:
            return lax.dynamic_slice_in_dim(held, start, width, 1)
        return jnp.concatenate(
            [
                lax.dynamic_slice_in_dim(held, start + (1 - low) * half, half, 1),
                lax.dynamic_slice_in_dim(held, start + low * half, half, 1),
            ],
            axis=1,
        )

    inputs = [columns(rank)]
    for s in range(1, n):
        piece = columns(rank ^ s)
        inputs.append(swap(piece, "ctx", s))

    def slope_terms(g, order, outs):
        col = lambda i: (0, 0, g)
        held_outs = [pl.BlockSpec(memory_space=pl.ANY)] * len(outs)
        count = 5 + 2 * n

        def body(*refs):
            slope_kernel(n, members, tokens, *refs[:count], *refs[count + len(outs) :])

        return pl.pallas_call(
            body,
            grid=(1,),
            in_specs=[smem]
            + [pl.BlockSpec((1, tokens, wide), col)] * 3
            + [pl.BlockSpec((1, members, tokens), lambda i: (0, g, 0))]
            + [pl.BlockSpec((1, tokens, HD), col)] * (2 * n)
            + held_outs,
            out_specs=[
                pl.BlockSpec((1, tokens, wide), col),
                pl.BlockSpec((n, tokens, HD), col),
            ],
            out_shape=[
                jax.ShapeDtypeStruct((1, tokens, groups * wide), BF16),
                jax.ShapeDtypeStruct((n, tokens, groups * HD), BF16),
            ],
            input_output_aliases={count + i: i for i in range(len(outs))},
            scratch_shapes=[
                pltpu.VMEM((n * tokens, members * tokens), BF16),
                pltpu.VMEM((1, members, tokens), F32),
            ],
        )(order, query_heads, output_grad, attention_out, log_norm, *keys, *values, *outs)

    vmem = pl.BlockSpec(memory_space=pltpu.VMEM)

    def weight_terms(x, got, turned):
        return pl.pallas_call(
            lambda *refs: weight_kernel(n, half, tokens, *refs),
            in_specs=[smem] + [vmem] * 3,
            out_shape=[
                jax.ShapeDtypeStruct((half, HD), BF16),
                jax.ShapeDtypeStruct((half, HD), BF16),
                jax.ShapeDtypeStruct((tokens, HD), BF16),
            ],
        )(meta, x, got, turned)

    sums = []
    for g in range(groups):
        sums.append(value_terms(g))
    outs = slope_terms(0, after(meta, sums[-1]), [])
    last = n // 2
    bit = 1
    while bit < last:
        got = []
        for g in range(groups):
            got.append(after(swap(sums[g], "ctx", bit), outs[1]))
        sums = [(x.astype(F32) + y.astype(F32)).astype(BF16) for x, y in zip(sums, got)]
        bit *= 2
    got = []
    for g in range(groups):
        got.append(swap(sums[g], "ctx", last))
    for g in range(1, groups):
        outs = slope_terms(g, after(meta, sums[-1]), outs)
    query_grad, key_terms = outs
    turned = pl.pallas_call(
        lambda *refs: turn_kernel(n, tokens, *refs),
        in_specs=[smem] + [vmem] * n,
        out_specs=vmem,
        out_shape=jax.ShapeDtypeStruct((width, n * tokens), BF16),
        name="turn",
    )(after(meta, key_terms), *inputs)

    own_rows, firsts, seconds = [], [], []
    for g in range(groups):
        first, second, own = weight_terms(sums[g], after(got[g], turned), turned)
        own_rows.append(own)
        firsts.append(first)
        seconds.append(second)
    value_rows = jnp.concatenate(own_rows, axis=1)
    value_grad = value_rows[None]

    mines = []
    for g in range(groups):
        if split_dp:
            part = swap(firsts[g], "dp", 1)
            mines.append((seconds[g].astype(F32) + part.astype(F32)).astype(BF16))
        else:
            mines.append(seconds[g])

    late_terms = after(key_terms, mines[-1])
    own_key = key_terms[0].astype(F32)
    for s in range(1, n):
        own_key = own_key + swap(late_terms[s], "ctx", s).astype(F32)
    key_grad = (own_key * (HD ** (-0.5))).astype(BF16)[None]

    tp_rank = lax.axis_index("tp")
    span = value_weight.shape[0] // tp

    def hidden_terms(owner):
        rows = lax.dynamic_slice_in_dim(value_weight, owner * span, span, 0)
        return jnp.einsum("te,de->td", late_rows, rows, preferred_element_type=F32)

    late_rows = after(value_rows, mines[0])

    received = [swap(hidden_terms(tp_rank ^ s).astype(BF16), "tp", s) for s in range(1, tp)]
    summed = hidden_terms(tp_rank)
    for r in received:
        summed = summed + r.astype(F32)
    hidden_grad = summed.astype(BF16)[None]

    def finish_dp(g):
        if not split_dp:
            return lax.psum(jnp.concatenate([firsts[g], mines[g]], axis=0), "dp").astype(F32)
        mine, bit = mines[g], 2
        while bit < dp:
            mine = (mine.astype(F32) + swap(mine, "dp", bit).astype(F32)).astype(BF16)
            bit *= 2
        other = swap(mine, "dp", 1)
        if g == groups - 1:
            other = after(other, hidden_grad, key_grad)
        return jnp.where(
            low == 0,
            jnp.concatenate([mine, other], axis=0),
            jnp.concatenate([other, mine], axis=0),
        ).astype(F32)

    token_norm = (dp * n * tokens) ** (-0.5)
    weight_grad = (
        jnp.concatenate([finish_dp(g) for g in range(groups)], axis=1) * token_norm
    )
    return (query_grad, key_grad, value_grad, hidden_grad, weight_grad)


def solution(mesh):
    placed = (
        P("dp", "ctx", None),
        P("dp", "ctx", "tp"),
        P("dp", "ctx", "tp"),
        P("dp", "ctx", "tp"),
        P("dp", "ctx", "tp"),
        P("dp", "ctx", "tp"),
        P("dp", "tp", "ctx"),
        P(),
        P(None, "tp"),
    )
    return jax.shard_map(
        shards,
        mesh=mesh,
        in_specs=placed,
        out_specs=(
            P("dp", "ctx", "tp"),
            P("dp", "ctx", "tp"),
            P("dp", "ctx", "tp"),
            P("dp", "ctx", "tp"),
            P("ctx", "tp"),
        ),
        check_vma=False,
    )
```

profile of v0, /device:TPU:0, one launch (start us, length us, event | category | flops | bytes accessed | tf_op | source)
XLA Modules:
  0.0 70.7 jit_solution(10693560728305413828)
XLA Ops:
  1.2 2.6 %collective-permute-start.1 = (bf16[1,128,256]{2,1,0:T(8,128)(2,1)}, bf16[1,128,256]{2,1,0:T(8,128)(2,1)S(1)}, u32[]{:S(2)}, u32[]{:S(2)}) collective-permute-start(bf16[1,128,256]{2,1,0:T(8,128)(2,1)} %refs_4_.7), channel_id=1, source_target_pairs={{0,4},{2,6},{4,0},{6,2},{1,5},{3,7},{5,1},{7,3},{8,12},{10,14},{12... | collective-permute-start | bytes 196616 | tf_op jit(solution)/shard_map/ppermute | solution.py:28
  4.0 1.9 %collective-permute-start.5 = (bf16[1,128,256]{2,1,0:T(8,128)(2,1)}, bf16[1,128,256]{2,1,0:T(8,128)(2,1)}, u32[]{:S(2)}, u32[]{:S(2)}) collective-permute-start(bf16[1,128,256]{2,1,0:T(8,128)(2,1)} %refs_9_.3), channel_id=1, source_target_pairs={{0,4},{2,6},{4,0},{6,2},{1,5},{3,7},{5,1},{7,3},{8,12},{10,14},{12... | collective-permute-start | bytes 196616 | tf_op jit(solution)/shard_map/ppermute | solution.py:28
  6.0 1.4 %dynamic-slice_bitcast_fusion.1 = (bf16[128,512]{1,0:T(8,128)(2,1)S(1)}, bf16[128,512]{1,0:T(8,128)(2,1)S(1)}, bf16[128,512]{1,0:T(8,128)(2,1)S(1)}, bf16[128,51...) fusion(bf16[1,128,4096]{2,1,0:T(8,128)(2,1)} %param.9, ...), kind=kLoop, calls=%fused_computation.25 | loop fusion | bytes 2097184 | tf_op jit(solution)/shard_map/dynamic_slice | solution.py:175
  7.4 0.7 %pad_maximum_fusion.1 = bf16[128,1024]{1,0:T(8,128)(2,1)} fusion(bf16[128,512]{1,0:T(8,128)(2,1)S(1)} %get-tuple-element.48, bf16[128,512]{1,0:T(8,128)(2,1)S(1)} %get-tuple-element.49), kind=kLoop, calls=%fused_computation.8 | loop fusion | flops 524288 | bytes 524288 | tf_op jit(solution)/shard_map/concatenate | solution.py:173
  10.0 2.7 %shard_map.132 = bf16[4,128,128]{2,1,0:T(8,128)(2,1)} custom-call(s32[9]{0:T(128)} %pad_add_fusion.refs_0_, bf16[1,128,2048]{2,1,0:T(8,128)(2,1)} %refs_1_.7, bf16[1,128,2048]{2,1,0:T(8,128)(2,1)} %refs_2_.7, f32[1,16,128]{2,1,0:T(8,128)} %refs_3_.7, bf16[1,128,256]{2,1,0:T(8,128)(2,1)} %refs_4_.7, bf16[1,128,256]{2,1,0:T(8,128)(2,1)} %copy-done.2, ...), custom_call_target="tpu_custom_call" | custom-call | tf_op jit(solution)/shard_map/pallas_call | solution.py:147
  12.9 2.7 %shard_map.128 = bf16[4,128,128]{2,1,0:T(8,128)(2,1)} custom-call(s32[9]{0:T(128)} %pad_add_fusion.refs_0_, bf16[1,128,2048]{2,1,0:T(8,128)(2,1)} %refs_1_.7, bf16[1,128,2048]{2,1,0:T(8,128)(2,1)} %refs_2_.7, f32[1,16,128]{2,1,0:T(8,128)} %refs_3_.7, bf16[1,128,256]{2,1,0:T(8,128)(2,1)} %refs_4_.7, bf16[1,128,256]{2,1,0:T(8,128)(2,1)} %copy-done.2, ...), custom_call_target="tpu_custom_call" | custom-call | tf_op jit(solution)/shard_map/pallas_call | solution.py:147
  15.9 0.7 %pad_maximum_fusion.2 = bf16[128,1024]{1,0:T(8,128)(2,1)} fusion(bf16[128,512]{1,0:T(8,128)(2,1)S(1)} %get-tuple-element.46, bf16[128,512]{1,0:T(8,128)(2,1)S(1)} %get-tuple-element.47), kind=kLoop, calls=%fused_computation.9 | loop fusion | flops 524288 | bytes 524288 | tf_op jit(solution)/shard_map/concatenate | solution.py:173
  18.1 1.6 %collective-permute-start.9 = (bf16[128,1024]{1,0:T(8,128)(2,1)}, bf16[128,1024]{1,0:T(8,128)(2,1)S(1)}, u32[]{:S(2)}, u32[]{:S(2)}) collective-permute-start(bf16[128,1024]{1,0:T(8,128)(2,1)} %pad_maximum_fusion.2), channel_id=1, source_target_pairs={{0,4},{2,6},{4,0},{6,2},{1,5},{3,7},{5,1},{7,3},{8,12},{10,14},{12... | collective-permute-start | bytes 786440 | tf_op jit(solution)/shard_map/ppermute | solution.py:28
  19.8 3.3 %shard_map.129 = (bf16[1,128,2048]{2,1,0:T(8,128)(2,1)}, bf16[4,128,256]{2,1,0:T(8,128)(2,1)}) custom-call(s32[9]{0:T(128)} %pad_add_fusion.refs_0_, bf16[1,128,2048]{2,1,0:T(8,128)(2,1)} %refs_1_.7, bf16[1,128,2048]{2,1,0:T(8,128)(2,1)} %refs_2_.7, bf16[1,128,2048]{2,1,0:T(8,128)(2,1)} %refs_3_.6, f32[1,16,128]{2,1,0:T(8,128)} %refs_3_.7, ...), custom_call_target="tpu_custom_call" | custom-call | tf_op jit(solution)/shard_map/pallas_call | solution.py:194
  23.2 0.9 %add_convert_fusion.6.refs_1_ = bf16[4,128,128]{2,1,0:T(8,128)(2,1)S(1)} fusion(bf16[4,128,128]{2,1,0:T(8,128)(2,1)} %collective-permute-done.3, bf16[4,128,128]{2,1,0:T(8,128)(2,1)S(1)} %copy-done.8), kind=kLoop, calls=%fused_computation.18 | loop fusion | flops 262144 | bytes 393216 | tf_op jit(solution)/shard_map/convert_element_type | solution.py:240
  24.1 1.7 %collective-permute-start.7 = (bf16[4,128,128]{2,1,0:T(8,128)(2,1)S(1)}, bf16[4,128,128]{2,1,0:T(8,128)(2,1)S(1)}, u32[]{:S(2)}, u32[]{:S(2)}) collective-permute-start(bf16[4,128,128]{2,1,0:T(8,128)(2,1)S(1)} %add_convert_fusion.6.refs_1_), channel_id=1, source_target_pairs={{0,4},{2,6},{4,0},{6,2},{1,5},{3,7},{5,1},{7,3},{8,12},{10,14},{12... | collective-permute-start | bytes 393224 | tf_op jit(solution)/shard_map/ppermute | solution.py:28
  25.9 0.9 %add_convert_fusion.4.refs_1_ = bf16[4,128,128]{2,1,0:T(8,128)(2,1)S(1)} fusion(bf16[4,128,128]{2,1,0:T(8,128)(2,1)} %collective-permute-done.15, bf16[4,128,128]{2,1,0:T(8,128)(2,1)S(1)} %copy-done.7), kind=kLoop, calls=%fused_computation.16 | loop fusion | flops 262144 | bytes 393216 | tf_op jit(solution)/shard_map/convert_element_type | solution.py:240
  28.0 3.3 %shard_map.130 = (bf16[1,128,2048]{2,1,0:T(8,128)(2,1)}, bf16[4,128,256]{2,1,0:T(8,128)(2,1)}) custom-call(s32[9]{0:T(128)} %pad_add_fusion.refs_0_, bf16[1,128,2048]{2,1,0:T(8,128)(2,1)} %refs_1_.7, bf16[1,128,2048]{2,1,0:T(8,128)(2,1)} %refs_2_.7, bf16[1,128,2048]{2,1,0:T(8,128)(2,1)} %refs_3_.6, ...), custom_call_target="tpu_custom_call", output_to_operand_aliasing={{0}: (13, {}), {1}: (14, {})} | custom-call | tf_op jit(solution)/shard_map/pallas_call | solution.py:194
  31.3 1.0 %collective-permute-done.10.refs_4_ = bf16[128,1024]{1,0:T(8,128)(2,1)} collective-permute-done((bf16[128,1024]{1,0:T(8,128)(2,1)}, bf16[128,1024]{1,0:T(8,128)(2,1)}, u32[]{:S(2)}, u32[]{:S(2)}) %collective-permute-start.10) | collective-permute-done | bytes 262176 | tf_op jit(solution)/shard_map/ppermute | solution.py:28
  32.3 2.5 %turn.1.refs_3_ = bf16[1024,512]{1,0:T(8,128)(2,1)} custom-call(s32[9]{0:T(128)} %pad_add_fusion.refs_0_, bf16[128,1024]{1,0:T(8,128)(2,1)} %pad_maximum_fusion.refs_1_, bf16[128,1024]{1,0:T(8,128)(2,1)} %copy-done.10, bf16[128,1024]{1,0:T(8,128)(2,1)} %copy-done.11, bf16[128,1024]{1,0:T(8,128)(2,1)} %collective-permute-done.10.refs_4_), custom_call_target="tpu_custom_call" | custom-call | tf_op jit(solution)/shard_map/turn/pallas_call | solution.py:248
  34.8 1.1 %collective-permute-done.7.refs_2_ = bf16[4,128,128]{2,1,0:T(8,128)(2,1)S(1)} collective-permute-done((bf16[4,128,128]{2,1,0:T(8,128)(2,1)S(1)}, bf16[4,128,128]{2,1,0:T(8,128)(2,1)S(1)}, u32[]{:S(2)}, u32[]{:S(2)}) %collective-permute-start.7) | collective-permute-done | bytes 131104 | tf_op jit(solution)/shard_map/ppermute | solution.py:28
  36.5 2.5 %shard_map.131 = (bf16[512,128]{1,0:T(8,128)(2,1)}, bf16[512,128]{1,0:T(8,128)(2,1)}, bf16[128,128]{1,0:T(8,128)(2,1)}) custom-call(s32[9]{0:T(128)} %pad_add_fusion.refs_0_, bf16[4,128,128]{2,1,0:T(8,128)(2,1)} %copy-done.6, bf16[4,128,128]{2,1,0:T(8,128)(2,1)} %copy-done.15, bf16[1024,512]{1,0:T(8,128)(2,1)} %turn.1.refs_3_), custom_call_target="tpu_custom_call" | custom-call | tf_op jit(solution)/shard_map/pallas_call | solution.py:220
  39.0 1.7 %collective-permute-start.11 = (bf16[512,128]{1,0:T(8,128)(2,1)}, bf16[512,128]{1,0:T(8,128)(2,1)S(1)}, u32[]{:S(2)}, u32[]{:S(2)}) collective-permute-start(bf16[512,128]{1,0:T(8,128)(2,1)} %get-tuple-element.35), channel_id=1, source_target_pairs={{0,8},{8,0},{16,24},{24,16},{1,9},{9,1},{17,25},{25,17},{2,10},{10... | collective-permute-start | bytes 393224 | tf_op jit(solution)/shard_map/ppermute | solution.py:28
  41.4 2.5 %shard_map.133 = (bf16[512,128]{1,0:T(8,128)(2,1)}, bf16[512,128]{1,0:T(8,128)(2,1)}, bf16[128,128]{1,0:T(8,128)(2,1)}) custom-call(s32[9]{0:T(128)} %pad_add_fusion.refs_0_, bf16[4,128,128]{2,1,0:T(8,128)(2,1)} %copy-done.5, bf16[4,128,128]{2,1,0:T(8,128)(2,1)} %copy-done.14, bf16[1024,512]{1,0:T(8,128)(2,1)} %turn.1.refs_3_), custom_call_target="tpu_custom_call" | custom-call | tf_op jit(solution)/shard_map/pallas_call | solution.py:220
  43.9 0.8 %constant_dynamic-update-slice_fusion.1 = bf16[128,256]{1,0:T(8,128)(2,1)S(1)} fusion(bf16[128,128]{1,0:T(8,128)(2,1)} %get-tuple-element.39), kind=kLoop, calls=%fused_computation.37 | loop fusion | bytes 65536
  45.0 0.8 %constant_dynamic-update-slice_fusion = bf16[128,256]{1,0:T(8,128)(2,1)S(1)} fusion(bf16[128,256]{1,0:T(8,128)(2,1)S(1)} %constant_dynamic-update-slice_fusion.1, bf16[128,128]{1,0:T(8,128)(2,1)} %get-tuple-element.40), kind=kLoop, calls=%fused_computation.36 | loop fusion | bytes 65536 | tf_op jit(solution)/shard_map/concatenate | solution.py:262
  45.8 1.0 %add_convert_fusion.5 = bf16[512,128]{1,0:T(8,128)(2,1)S(1)} fusion(bf16[512,128]{1,0:T(8,128)(2,1)S(1)} %collective-permute-done.11, bf16[512,128]{1,0:T(8,128)(2,1)} %get-tuple-element.34), kind=kLoop, calls=%fused_computation.17 | loop fusion | flops 262144 | bytes 393216 | tf_op jit(solution)/shard_map/convert_element_type | solution.py:269
  46.8 2.8 %collective-permute-start.21 = (bf16[512,128]{1,0:T(8,128)(2,1)S(1)}, bf16[512,128]{1,0:T(8,128)(2,1)S(1)}, u32[]{:S(2)}, u32[]{:S(2)}) collective-permute-start(bf16[512,128]{1,0:T(8,128)(2,1)S(1)} %add_convert_fusion.5), channel_id=1, source_target_pairs={{0,16},{8,24},{16,0},{24,8},{1,17},{9,25},{17,1},{25,9},{2,18},{10... | collective-permute-start | bytes 393224 | tf_op jit(solution)/shard_map/ppermute | solution.py:28
  49.6 1.6 %collective-permute-start.13 = (bf16[128,256]{1,0:T(8,128)(2,1)S(1)}, bf16[128,256]{1,0:T(8,128)(2,1)S(1)}, u32[]{:S(2)}, u32[]{:S(2)}) collective-permute-start(bf16[128,256]{1,0:T(8,128)(2,1)S(1)} %get-tuple-element.55), channel_id=1, source_target_pairs={{0,4},{2,6},{4,0},{6,2},{1,5},{3,7},{5,1},{7,3},{8,12},{10,14},{12... | collective-permute-start | bytes 196616 | tf_op jit(solution)/shard_map/ppermute | solution.py:28
  51.5 0.9 %add_convert_fusion.3 = bf16[512,128]{1,0:T(8,128)(2,1)S(1)} fusion(bf16[512,128]{1,0:T(8,128)(2,1)S(1)} %collective-permute-done.17, bf16[512,128]{1,0:T(8,128)(2,1)} %get-tuple-element.41), kind=kLoop, calls=%fused_computation.15 | loop fusion | flops 262144 | bytes 393216 | tf_op jit(solution)/shard_map/convert_element_type | solution.py:269
  52.4 2.4 %collective-permute-start.19 = (bf16[512,128]{1,0:T(8,128)(2,1)S(1)}, bf16[512,128]{1,0:T(8,128)(2,1)S(1)}, u32[]{:S(2)}, u32[]{:S(2)}) collective-permute-start(bf16[512,128]{1,0:T(8,128)(2,1)S(1)} %add_convert_fusion.3), channel_id=1, source_target_pairs={{0,16},{8,24},{16,0},{24,8},{1,17},{9,25},{17,1},{25,9},{2,18},{10... | collective-permute-start | bytes 393224 | tf_op jit(solution)/shard_map/ppermute | solution.py:28
  55.3 1.6 %collective-permute-start.18 = (bf16[128,2048]{1,0:T(8,128)(2,1)S(1)}, bf16[128,2048]{1,0:T(8,128)(2,1)S(1)}, u32[]{:S(2)}, u32[]{:S(2)}) collective-permute-start(bf16[128,2048]{1,0:T(8,128)(2,1)S(1)} %convolution_convert_fusion), channel_id=1, source_target_pairs={{0,1},{1,0},{2,3},{3,2},{4,5},{5,4},{6,7},{7,6},{8,9},{9,8},{10,11... | collective-permute-start | bytes 1572872 | tf_op jit(solution)/shard_map/ppermute | solution.py:28
  57.5 4.3 %collective-permute-done.19 = bf16[512,128]{1,0:T(8,128)(2,1)S(1)} collective-permute-done((bf16[512,128]{1,0:T(8,128)(2,1)S(1)}, bf16[512,128]{1,0:T(8,128)(2,1)S(1)}, u32[]{:S(2)}, u32[]{:S(2)}) %collective-permute-start.19) | collective-permute-done | bytes 131104 | tf_op jit(solution)/shard_map/ppermute | solution.py:28
  62.0 2.1 %collective-permute-start.22 = (bf16[512,128]{1,0:T(8,128)(2,1)S(1)}, bf16[512,128]{1,0:T(8,128)(2,1)S(1)}, u32[]{:S(2)}, u32[]{:S(2)}) collective-permute-start(bf16[512,128]{1,0:T(8,128)(2,1)S(1)} %add_convert_fusion.1), channel_id=1, source_target_pairs={{0,8},{8,0},{16,24},{24,16},{1,9},{9,1},{17,25},{25,17},{2,10},{10... | collective-permute-start | bytes 393224 | tf_op jit(solution)/shard_map/ppermute | solution.py:28
  64.1 4.1 %collective-permute-done.20 = bf16[512,128]{1,0:T(8,128)(2,1)S(1)} collective-permute-done((bf16[512,128]{1,0:T(8,128)(2,1)S(1)}, bf16[512,128]{1,0:T(8,128)(2,1)S(1)}, u32[]{:S(2)}, u32[]{:S(2)}) %collective-permute-start.20) | collective-permute-done | bytes 131104 | tf_op jit(solution)/shard_map/ppermute | solution.py:28
  68.2 1.3 %fusion.5 = bf16[1,128,2048]{2,1,0:T(8,128)(2,1)} fusion(bf16[128,2048]{1,0:T(8,128)(2,1)S(1)} %collective-permute-done.18, bf16[128,256]{1,0:T(8,128)(2,1)S(1)} %constant_dynamic-update-slice_fusion, bf16[4096,256]{1,0:T(8,128)(2,1)S(1)} %copy-done, s32[]{:T(128)S(6)} %select_n.58), kind=kOutput, calls=%fused_computation.6 | convolution fusion | flops 135004160 | bytes 2162692 | tf_op jit(solution)/shard_map/te,de->td/dot_general | solution.py:284
  69.6 1.1 %convert_multiply_fusion = f32[1024,256]{1,0:T(8,128)} fusion(bf16[1024,128]{1,0:T(8,128)(2,1)S(1)} %maximum_select_fusion.1, bf16[1024,128]{1,0:T(8,128)(2,1)S(1)} %maximum_select_fusion), kind=kLoop, calls=%fused_computation.1 | loop fusion | flops 1310720 | bytes 1572864 | tf_op jit(solution)/shard_map/mul | solution.py:312
  (76 shorter events, 9.4 us)
Async XLA Ops:
  0.6 54.2 %copy-start = (bf16[4096,256]{1,0:T(8,128)(2,1)S(1)}, bf16[4096,256]{1,0:T(8,128)(2,1)}, u32[]{:S(2)}) copy-start(bf16[4096,256]{1,0:T(8,128)(2,1)} %param.17) | copy-start | bytes 6291460
  0.6 8.0 %copy-start.12 = (bf16[1,128,256]{2,1,0:T(8,128)(2,1)S(1)}, bf16[1,128,256]{2,1,0:T(8,128)(2,1)}, u32[]{:S(2)}) copy-start(bf16[1,128,256]{2,1,0:T(8,128)(2,1)} %refs_9_.3) | copy-start | bytes 196612
  0.7 7.4 %copy-start.16 = (s32[8]{0:T(128)S(1)}, s32[8]{0:T(128)}, u32[]{:S(2)}) copy-start(s32[8]{0:T(128)} %param.16) | copy-start | bytes 100
  0.7 8.0 %collective-permute-start = (bf16[1,128,256]{2,1,0:T(8,128)(2,1)}, bf16[1,128,256]{2,1,0:T(8,128)(2,1)S(1)}, u32[]{:S(2)}, u32[]{:S(2)}) collective-permute-start(bf16[1,128,256]{2,1,0:T(8,128)(2,1)} %refs_4_.7), channel_id=1, source_target_pairs={{0,2},{2,0},{4,6},{6,4},{1,3},{3,1},{5,7},{7,5},{8,10},{10,8},{12,... | collective-permute-start | bytes 196616 | tf_op jit(solution)/shard_map/ppermute | solution.py:28
  1.2 7.5 %collective-permute-start.1 = (bf16[1,128,256]{2,1,0:T(8,128)(2,1)}, bf16[1,128,256]{2,1,0:T(8,128)(2,1)S(1)}, u32[]{:S(2)}, u32[]{:S(2)}) collective-permute-start(bf16[1,128,256]{2,1,0:T(8,128)(2,1)} %refs_4_.7), channel_id=1, source_target_pairs={{0,4},{2,6},{4,0},{6,2},{1,5},{3,7},{5,1},{7,3},{8,12},{10,14},{12... | collective-permute-start | bytes 196616 | tf_op jit(solution)/shard_map/ppermute | solution.py:28
  3.8 5.0 %collective-permute-start.2 = (bf16[1,128,256]{2,1,0:T(8,128)(2,1)}, bf16[1,128,256]{2,1,0:T(8,128)(2,1)S(1)}, u32[]{:S(2)}, u32[]{:S(2)}) collective-permute-start(bf16[1,128,256]{2,1,0:T(8,128)(2,1)} %refs_4_.7), channel_id=1, source_target_pairs={{0,6},{2,4},{4,2},{6,0},{1,7},{3,5},{5,3},{7,1},{8,14},{10,12},{12... | collective-permute-start | bytes 196616 | tf_op jit(solution)/shard_map/ppermute | solution.py:28
  3.8 13.6 %collective-permute-start.4 = (bf16[1,128,256]{2,1,0:T(8,128)(2,1)}, bf16[1,128,256]{2,1,0:T(8,128)(2,1)S(1)}, u32[]{:S(2)}, u32[]{:S(2)}) collective-permute-start(bf16[1,128,256]{2,1,0:T(8,128)(2,1)} %refs_9_.3), channel_id=1, source_target_pairs={{0,2},{2,0},{4,6},{6,4},{1,3},{3,1},{5,7},{7,5},{8,10},{10,8},{12,... | collective-permute-start | bytes 196616 | tf_op jit(solution)/shard_map/ppermute | solution.py:28
  4.0 14.0 %collective-permute-start.5 = (bf16[1,128,256]{2,1,0:T(8,128)(2,1)}, bf16[1,128,256]{2,1,0:T(8,128)(2,1)}, u32[]{:S(2)}, u32[]{:S(2)}) collective-permute-start(bf16[1,128,256]{2,1,0:T(8,128)(2,1)} %refs_9_.3), channel_id=1, source_target_pairs={{0,4},{2,6},{4,0},{6,2},{1,5},{3,7},{5,1},{7,3},{8,12},{10,14},{12... | collective-permute-start | bytes 196616 | tf_op jit(solution)/shard_map/ppermute | solution.py:28
  8.7 11.0 %collective-permute-start.6 = (bf16[1,128,256]{2,1,0:T(8,128)(2,1)S(1)}, bf16[1,128,256]{2,1,0:T(8,128)(2,1)}, u32[]{:S(2)}, u32[]{:S(2)}) collective-permute-start(bf16[1,128,256]{2,1,0:T(8,128)(2,1)S(1)} %copy-done.12), channel_id=1, source_target_pairs={{0,6},{2,4},{4,2},{6,0},{1,7},{3,5},{5,3},{7,1},{8,14},{10,12},{12... | collective-permute-start | bytes 196616 | tf_op jit(solution)/shard_map/ppermute | solution.py:28
  12.7 10.4 %collective-permute-start.15 = (bf16[4,128,128]{2,1,0:T(8,128)(2,1)}, bf16[4,128,128]{2,1,0:T(8,128)(2,1)}, u32[]{:S(2)}, u32[]{:S(2)}) collective-permute-start(bf16[4,128,128]{2,1,0:T(8,128)(2,1)} %shard_map.132), channel_id=1, source_target_pairs={{0,2},{2,0},{4,6},{6,4},{1,3},{3,1},{5,7},{7,5},{8,10},{10,8},{12,... | collective-permute-start | bytes 393224 | tf_op jit(solution)/shard_map/ppermute | solution.py:28
  15.6 7.6 %copy-start.8 = (bf16[4,128,128]{2,1,0:T(8,128)(2,1)S(1)}, bf16[4,128,128]{2,1,0:T(8,128)(2,1)}, u32[]{:S(2)}) copy-start(bf16[4,128,128]{2,1,0:T(8,128)(2,1)} %shard_map.128) | copy-start | bytes 393220
  15.6 10.3 %copy-start.7 = (bf16[4,128,128]{2,1,0:T(8,128)(2,1)S(1)}, bf16[4,128,128]{2,1,0:T(8,128)(2,1)}, u32[]{:S(2)}) copy-start(bf16[4,128,128]{2,1,0:T(8,128)(2,1)} %shard_map.132) | copy-start | bytes 393220
  15.6 7.6 %collective-permute-start.3 = (bf16[4,128,128]{2,1,0:T(8,128)(2,1)}, bf16[4,128,128]{2,1,0:T(8,128)(2,1)}, u32[]{:S(2)}, u32[]{:S(2)}) collective-permute-start(bf16[4,128,128]{2,1,0:T(8,128)(2,1)} %shard_map.128), channel_id=1, source_target_pairs={{0,2},{2,0},{4,6},{6,4},{1,3},{3,1},{5,7},{7,5},{8,10},{10,8},{12,... | collective-permute-start | bytes 393224 | tf_op jit(solution)/shard_map/ppermute | solution.py:28
  17.4 13.9 %collective-permute-start.8 = (bf16[128,1024]{1,0:T(8,128)(2,1)}, bf16[128,1024]{1,0:T(8,128)(2,1)S(1)}, u32[]{:S(2)}, u32[]{:S(2)}) collective-permute-start(bf16[128,1024]{1,0:T(8,128)(2,1)} %pad_maximum_fusion.1), channel_id=1, source_target_pairs={{0,2},{2,0},{4,6},{6,4},{1,3},{3,1},{5,7},{7,5},{8,10},{10,8},{12,... | collective-permute-start | bytes 786440 | tf_op jit(solution)/shard_map/ppermute | solution.py:28
  18.1 13.3 %collective-permute-start.9 = (bf16[128,1024]{1,0:T(8,128)(2,1)}, bf16[128,1024]{1,0:T(8,128)(2,1)S(1)}, u32[]{:S(2)}, u32[]{:S(2)}) collective-permute-start(bf16[128,1024]{1,0:T(8,128)(2,1)} %pad_maximum_fusion.2), channel_id=1, source_target_pairs={{0,4},{2,6},{4,0},{6,2},{1,5},{3,7},{5,1},{7,3},{8,12},{10,14},{12... | collective-permute-start | bytes 786440 | tf_op jit(solution)/shard_map/ppermute | solution.py:28
  19.7 12.6 %collective-permute-start.10 = (bf16[128,1024]{1,0:T(8,128)(2,1)}, bf16[128,1024]{1,0:T(8,128)(2,1)}, u32[]{:S(2)}, u32[]{:S(2)}) collective-permute-start(bf16[128,1024]{1,0:T(8,128)(2,1)} %pad_maximum_fusion.3), channel_id=1, source_target_pairs={{0,6},{2,4},{4,2},{6,0},{1,7},{3,5},{5,3},{7,1},{8,14},{10,12},{12... | collective-permute-start | bytes 786440 | tf_op jit(solution)/shard_map/ppermute | solution.py:28
  24.1 10.7 %copy-start.6 = (bf16[4,128,128]{2,1,0:T(8,128)(2,1)}, bf16[4,128,128]{2,1,0:T(8,128)(2,1)S(1)}, u32[]{:S(2)}) copy-start(bf16[4,128,128]{2,1,0:T(8,128)(2,1)S(1)} %add_convert_fusion.6.refs_1_) | copy-start | bytes 393220
  24.1 11.7 %collective-permute-start.7 = (bf16[4,128,128]{2,1,0:T(8,128)(2,1)S(1)}, bf16[4,128,128]{2,1,0:T(8,128)(2,1)S(1)}, u32[]{:S(2)}, u32[]{:S(2)}) collective-permute-start(bf16[4,128,128]{2,1,0:T(8,128)(2,1)S(1)} %add_convert_fusion.6.refs_1_), channel_id=1, source_target_pairs={{0,4},{2,6},{4,0},{6,2},{1,5},{3,7},{5,1},{7,3},{8,12},{10,14},{12... | collective-permute-start | bytes 393224 | tf_op jit(solution)/shard_map/ppermute | solution.py:28
  26.8 8.0 %copy-start.5 = (bf16[4,128,128]{2,1,0:T(8,128)(2,1)}, bf16[4,128,128]{2,1,0:T(8,128)(2,1)S(1)}, u32[]{:S(2)}) copy-start(bf16[4,128,128]{2,1,0:T(8,128)(2,1)S(1)} %add_convert_fusion.4.refs_1_) | copy-start | bytes 393220
  26.8 13.9 %collective-permute-start.16 = (bf16[4,128,128]{2,1,0:T(8,128)(2,1)S(1)}, bf16[4,128,128]{2,1,0:T(8,128)(2,1)S(1)}, u32[]{:S(2)}, u32[]{:S(2)}) collective-permute-start(bf16[4,128,128]{2,1,0:T(8,128)(2,1)S(1)} %add_convert_fusion.4.refs_1_), channel_id=1, source_target_pairs={{0,4},{2,6},{4,0},{6,2},{1,5},{3,7},{5,1},{7,3},{8,12},{10,14},{12... | collective-permute-start | bytes 393224 | tf_op jit(solution)/shard_map/ppermute | solution.py:28
  34.8 14.7 %copy-start.1 = (bf16[4,128,256]{2,1,0:T(8,128)(2,1)S(1)}, bf16[4,128,256]{2,1,0:T(8,128)(2,1)}, u32[]{:S(2)}) copy-start(bf16[4,128,256]{2,1,0:T(8,128)(2,1)} %get-tuple-element.36) | copy-start | bytes 786436
  39.0 6.7 %collective-permute-start.11 = (bf16[512,128]{1,0:T(8,128)(2,1)}, bf16[512,128]{1,0:T(8,128)(2,1)S(1)}, u32[]{:S(2)}, u32[]{:S(2)}) collective-permute-start(bf16[512,128]{1,0:T(8,128)(2,1)} %get-tuple-element.35), channel_id=1, source_target_pairs={{0,8},{8,0},{16,24},{24,16},{1,9},{9,1},{17,25},{25,17},{2,10},{10... | collective-permute-start | bytes 393224 | tf_op jit(solution)/shard_map/ppermute | solution.py:28
  44.7 6.8 %collective-permute-start.17 = (bf16[512,128]{1,0:T(8,128)(2,1)}, bf16[512,128]{1,0:T(8,128)(2,1)S(1)}, u32[]{:S(2)}, u32[]{:S(2)}) collective-permute-start(bf16[512,128]{1,0:T(8,128)(2,1)} %get-tuple-element.42), channel_id=1, source_target_pairs={{0,8},{8,0},{16,24},{24,16},{1,9},{9,1},{17,25},{25,17},{2,10},{10... | collective-permute-start | bytes 393224 | tf_op jit(solution)/shard_map/ppermute | solution.py:28
  45.8 22.5 %copy-start.9 = (bf16[128,256]{1,0:T(8,128)(2,1)}, bf16[128,256]{1,0:T(8,128)(2,1)S(1)}, u32[]{:S(2)}) copy-start(bf16[128,256]{1,0:T(8,128)(2,1)S(1)} %constant_dynamic-update-slice_fusion) | copy-start | bytes 196612
  46.8 15.2 %collective-permute-start.21 = (bf16[512,128]{1,0:T(8,128)(2,1)S(1)}, bf16[512,128]{1,0:T(8,128)(2,1)S(1)}, u32[]{:S(2)}, u32[]{:S(2)}) collective-permute-start(bf16[512,128]{1,0:T(8,128)(2,1)S(1)} %add_convert_fusion.5), channel_id=1, source_target_pairs={{0,16},{8,24},{16,0},{24,8},{1,17},{9,25},{17,1},{25,9},{2,18},{10... | collective-permute-start | bytes 393224 | tf_op jit(solution)/shard_map/ppermute | solution.py:28
  49.5 5.7 %collective-permute-start.14 = (bf16[128,256]{1,0:T(8,128)(2,1)S(1)}, bf16[128,256]{1,0:T(8,128)(2,1)S(1)}, u32[]{:S(2)}, u32[]{:S(2)}) collective-permute-start(bf16[128,256]{1,0:T(8,128)(2,1)S(1)} %get-tuple-element.54), channel_id=1, source_target_pairs={{0,6},{2,4},{4,2},{6,0},{1,7},{3,5},{5,3},{7,1},{8,14},{10,12},{12... | collective-permute-start | bytes 196616 | tf_op jit(solution)/shard_map/ppermute | solution.py:28
  49.6 7.2 %collective-permute-start.13 = (bf16[128,256]{1,0:T(8,128)(2,1)S(1)}, bf16[128,256]{1,0:T(8,128)(2,1)S(1)}, u32[]{:S(2)}, u32[]{:S(2)}) collective-permute-start(bf16[128,256]{1,0:T(8,128)(2,1)S(1)} %get-tuple-element.55), channel_id=1, source_target_pairs={{0,4},{2,6},{4,0},{6,2},{1,5},{3,7},{5,1},{7,3},{8,12},{10,14},{12... | collective-permute-start | bytes 196616 | tf_op jit(solution)/shard_map/ppermute | solution.py:28
  51.2 5.6 %collective-permute-start.12 = (bf16[128,256]{1,0:T(8,128)(2,1)S(1)}, bf16[128,256]{1,0:T(8,128)(2,1)S(1)}, u32[]{:S(2)}, u32[]{:S(2)}) collective-permute-start(bf16[128,256]{1,0:T(8,128)(2,1)S(1)} %get-tuple-element.53), channel_id=1, source_target_pairs={{0,2},{2,0},{4,6},{6,4},{1,3},{3,1},{5,7},{7,5},{8,10},{10,8},{12,... | collective-permute-start | bytes 196616 | tf_op jit(solution)/shard_map/ppermute | solution.py:28
  52.4 9.4 %collective-permute-start.19 = (bf16[512,128]{1,0:T(8,128)(2,1)S(1)}, bf16[512,128]{1,0:T(8,128)(2,1)S(1)}, u32[]{:S(2)}, u32[]{:S(2)}) collective-permute-start(bf16[512,128]{1,0:T(8,128)(2,1)S(1)} %add_convert_fusion.3), channel_id=1, source_target_pairs={{0,16},{8,24},{16,0},{24,8},{1,17},{9,25},{17,1},{25,9},{2,18},{10... | collective-permute-start | bytes 393224 | tf_op jit(solution)/shard_map/ppermute | solution.py:28
  55.3 12.9 %collective-permute-start.18 = (bf16[128,2048]{1,0:T(8,128)(2,1)S(1)}, bf16[128,2048]{1,0:T(8,128)(2,1)S(1)}, u32[]{:S(2)}, u32[]{:S(2)}) collective-permute-start(bf16[128,2048]{1,0:T(8,128)(2,1)S(1)} %convolution_convert_fusion), channel_id=1, source_target_pairs={{0,1},{1,0},{2,3},{3,2},{4,5},{5,4},{6,7},{7,6},{8,9},{9,8},{10,11... | collective-permute-start | bytes 1572872 | tf_op jit(solution)/shard_map/ppermute | solution.py:28
  61.9 6.3 %collective-permute-start.20 = (bf16[512,128]{1,0:T(8,128)(2,1)S(1)}, bf16[512,128]{1,0:T(8,128)(2,1)S(1)}, u32[]{:S(2)}, u32[]{:S(2)}) collective-permute-start(bf16[512,128]{1,0:T(8,128)(2,1)S(1)} %add_convert_fusion.2), channel_id=1, source_target_pairs={{0,8},{8,0},{16,24},{24,16},{1,9},{9,1},{17,25},{25,17},{2,10},{10... | collective-permute-start | bytes 393224 | tf_op jit(solution)/shard_map/ppermute | solution.py:28
  62.0 7.5 %collective-permute-start.22 = (bf16[512,128]{1,0:T(8,128)(2,1)S(1)}, bf16[512,128]{1,0:T(8,128)(2,1)S(1)}, u32[]{:S(2)}, u32[]{:S(2)}) collective-permute-start(bf16[512,128]{1,0:T(8,128)(2,1)S(1)} %add_convert_fusion.1), channel_id=1, source_target_pairs={{0,8},{8,0},{16,24},{24,16},{1,9},{9,1},{17,25},{25,17},{2,10},{10... | collective-permute-start | bytes 393224 | tf_op jit(solution)/shard_map/ppermute | solution.py:28
  (8 other events, 5.8 us)
where the time goes:
time: 71.2 us; the launch traced here: 70.7 us
  starting transfers between devices  22.7 us (32%)
  Pallas kernels  19.6 us (28%)
  waiting for transfers between devices  10.5 us (15%)
  other arithmetic  9.26 us (13%)
  local copies, waits for them, and re-layouts  5.98 us (8%)
  matrix products  1.75 us (2%)
  between operations  0.9 us (1%)
    ppermute x23, starting transfers between devices, swap(): return lax.ppermute(x, axis, [(i, i ^ s) for i in range(n)])  22.7 us
    ppermute x23, waiting for transfers between devices, swap(): return lax.ppermute(x, axis, [(i, i ^ s) for i in range(n)])  10.5 us
    pallas_call x2, Pallas kernels, slope_terms(): pl.pallas_call(body, grid=(1,), in_specs=[smem] + [pl.BlockSpec((1, token...  6.63 us
    pallas_call x2, Pallas kernels, value_terms(): pl.pallas_call(lambda *refs: value_kernel(n, members, tokens, *refs), gri...  5.42 us
    pallas_call x2, Pallas kernels, weight_terms(): pl.pallas_call(lambda *refs: weight_kernel(n, half, tokens, *refs), in_sp...  5.05 us
    unnamed x35, local copies, waits for them, and re-layouts  3.8 us
    concatenate x4, other arithmetic, columns(): jnp.concatenate([lax.dynamic_slice_in_dim(held, start + (1 - low) * half,...  2.93 us
    pallas_call x1, Pallas kernels, shards(): pl.pallas_call(lambda *refs: turn_kernel(n, tokens, *refs), in_specs=[sme...  2.49 us
  transfers between devices with their start and end apart: 23, of which 4 were waited for; matrix products, arithmetic and copies ran while one was open for 18% of the time, Pallas kernels for 28%

commit v1 on v0

--- a/solution.py
+++ b/solution.py
@@ -273,7 +273,8 @@
     late_terms = after(key_terms, mines[-1])
     own_key = key_terms[0].astype(F32)
     for s in range(1, n):
-        own_key = own_key + swap(late_terms[s], "ctx", s).astype(F32)
+        part = swap(late_terms[s], "ctx", s)
+        own_key = own_key + part.astype(F32)
     key_grad = (own_key * (HD ** (-0.5))).astype(BF16)[None]
 
     tp_rank = lax.axis_index("tp")
@@ -285,7 +286,10 @@
 
     late_rows = after(value_rows, mines[0])
 
-    received = [swap(hidden_terms(tp_rank ^ s).astype(BF16), "tp", s) for s in range(1, tp)]
+    received = []
+    for s in range(1, tp):
+        part = hidden_terms(tp_rank ^ s).astype(BF16)
+        received.append(swap(part, "tp", s))
     summed = hidden_terms(tp_rank)
     for r in received:
         summed = summed + r.astype(F32)
@@ -296,7 +300,8 @@
             return lax.psum(jnp.concatenate([firsts[g], mines[g]], axis=0), "dp").astype(F32)
         mine, bit = mines[g], 2
         while bit < dp:
-            mine = (mine.astype(F32) + swap(mine, "dp", bit).astype(F32)).astype(BF16)
+            across = swap(mine, "dp", bit)
+            mine = (mine.astype(F32) + across.astype(F32)).astype(BF16)
             bit *= 2
         other = swap(mine, "dp", 1)
         if g == groups - 1:

time: 71.2 us -> 71.2 us (level)
  no operation moved by 1% of the time
where the time goes in v1:
time: 71.2 us; the launch traced here: 70.7 us
  starting transfers between devices  22.7 us (32%)
  Pallas kernels  19.6 us (28%)
  waiting for transfers between devices  10.5 us (15%)
  other arithmetic  9.26 us (13%)
  local copies, waits for them, and re-layouts  5.98 us (8%)
  matrix products  1.75 us (2%)
  between operations  0.9 us (1%)
    ppermute x23, starting transfers between devices, swap(): return lax.ppermute(x, axis, [(i, i ^ s) for i in range(n)])  22.7 us
    ppermute x23, waiting for transfers between devices, swap(): return lax.ppermute(x, axis, [(i, i ^ s) for i in range(n)])  10.5 us
    pallas_call x2, Pallas kernels, slope_terms(): pl.pallas_call(body, grid=(1,), in_specs=[smem] + [pl.BlockSpec((1, token...  6.63 us
    pallas_call x2, Pallas kernels, value_terms(): pl.pallas_call(lambda *refs: value_kernel(n, members, tokens, *refs), gri...  5.42 us
    pallas_call x2, Pallas kernels, weight_terms(): pl.pallas_call(lambda *refs: weight_kernel(n, half, tokens, *refs), in_sp...  5.05 us
    unnamed x35, local copies, waits for them, and re-layouts  3.8 us
    concatenate x4, other arithmetic, columns(): jnp.concatenate([lax.dynamic_slice_in_dim(held, start + (1 - low) * half,...  2.93 us
    pallas_call x1, Pallas kernels, shards(): pl.pallas_call(lambda *refs: turn_kernel(n, tokens, *refs), in_specs=[sme...  2.49 us
  transfers between devices with their start and end apart: 23, of which 4 were waited for; matrix products, arithmetic and copies ran while one was open for 18% of the time, Pallas kernels for 28%

profile of v1, /device:TPU:0, one launch (start us, length us, event | category | flops | bytes accessed | tf_op | source)
XLA Modules:
  0.0 70.7 jit_solution(10693560728305413828)
XLA Ops:
  1.2 2.6 %collective-permute-start.1 = (bf16[1,128,256]{2,1,0:T(8,128)(2,1)}, bf16[1,128,256]{2,1,0:T(8,128)(2,1)S(1)}, u32[]{:S(2)}, u32[]{:S(2)}) collective-permute-start(bf16[1,128,256]{2,1,0:T(8,128)(2,1)} %refs_4_.7), channel_id=1, source_target_pairs={{0,4},{2,6},{4,0},{6,2},{1,5},{3,7},{5,1},{7,3},{8,12},{10,14},{12... | collective-permute-start | bytes 196616 | tf_op jit(solution)/shard_map/ppermute | solution.py:28
  4.0 1.9 %collective-permute-start.5 = (bf16[1,128,256]{2,1,0:T(8,128)(2,1)}, bf16[1,128,256]{2,1,0:T(8,128)(2,1)}, u32[]{:S(2)}, u32[]{:S(2)}) collective-permute-start(bf16[1,128,256]{2,1,0:T(8,128)(2,1)} %refs_9_.3), channel_id=1, source_target_pairs={{0,4},{2,6},{4,0},{6,2},{1,5},{3,7},{5,1},{7,3},{8,12},{10,14},{12... | collective-permute-start | bytes 196616 | tf_op jit(solution)/shard_map/ppermute | solution.py:28
  6.0 1.4 %dynamic-slice_bitcast_fusion.1 = (bf16[128,512]{1,0:T(8,128)(2,1)S(1)}, bf16[128,512]{1,0:T(8,128)(2,1)S(1)}, bf16[128,512]{1,0:T(8,128)(2,1)S(1)}, bf16[128,51...) fusion(bf16[1,128,4096]{2,1,0:T(8,128)(2,1)} %param.9, ...), kind=kLoop, calls=%fused_computation.25 | loop fusion | bytes 2097184 | tf_op jit(solution)/shard_map/dynamic_slice | solution.py:175
  7.4 0.7 %pad_maximum_fusion.1 = bf16[128,1024]{1,0:T(8,128)(2,1)} fusion(bf16[128,512]{1,0:T(8,128)(2,1)S(1)} %get-tuple-element.48, bf16[128,512]{1,0:T(8,128)(2,1)S(1)} %get-tuple-element.49), kind=kLoop, calls=%fused_computation.8 | loop fusion | flops 524288 | bytes 524288 | tf_op jit(solution)/shard_map/concatenate | solution.py:173
  10.0 2.7 %shard_map.132 = bf16[4,128,128]{2,1,0:T(8,128)(2,1)} custom-call(s32[9]{0:T(128)} %pad_add_fusion.refs_0_, bf16[1,128,2048]{2,1,0:T(8,128)(2,1)} %refs_1_.7, bf16[1,128,2048]{2,1,0:T(8,128)(2,1)} %refs_2_.7, f32[1,16,128]{2,1,0:T(8,128)} %refs_3_.7, bf16[1,128,256]{2,1,0:T(8,128)(2,1)} %refs_4_.7, bf16[1,128,256]{2,1,0:T(8,128)(2,1)} %copy-done.2, ...), custom_call_target="tpu_custom_call" | custom-call | tf_op jit(solution)/shard_map/pallas_call | solution.py:147
  12.9 2.7 %shard_map.128 = bf16[4,128,128]{2,1,0:T(8,128)(2,1)} custom-call(s32[9]{0:T(128)} %pad_add_fusion.refs_0_, bf16[1,128,2048]{2,1,0:T(8,128)(2,1)} %refs_1_.7, bf16[1,128,2048]{2,1,0:T(8,128)(2,1)} %refs_2_.7, f32[1,16,128]{2,1,0:T(8,128)} %refs_3_.7, bf16[1,128,256]{2,1,0:T(8,128)(2,1)} %refs_4_.7, bf16[1,128,256]{2,1,0:T(8,128)(2,1)} %copy-done.2, ...), custom_call_target="tpu_custom_call" | custom-call | tf_op jit(solution)/shard_map/pallas_call | solution.py:147
  15.9 0.7 %pad_maximum_fusion.2 = bf16[128,1024]{1,0:T(8,128)(2,1)} fusion(bf16[128,512]{1,0:T(8,128)(2,1)S(1)} %get-tuple-element.46, bf16[128,512]{1,0:T(8,128)(2,1)S(1)} %get-tuple-element.47), kind=kLoop, calls=%fused_computation.9 | loop fusion | flops 524288 | bytes 524288 | tf_op jit(solution)/shard_map/concatenate | solution.py:173
  18.1 1.6 %collective-permute-start.9 = (bf16[128,1024]{1,0:T(8,128)(2,1)}, bf16[128,1024]{1,0:T(8,128)(2,1)S(1)}, u32[]{:S(2)}, u32[]{:S(2)}) collective-permute-start(bf16[128,1024]{1,0:T(8,128)(2,1)} %pad_maximum_fusion.2), channel_id=1, source_target_pairs={{0,4},{2,6},{4,0},{6,2},{1,5},{3,7},{5,1},{7,3},{8,12},{10,14},{12... | collective-permute-start | bytes 786440 | tf_op jit(solution)/shard_map/ppermute | solution.py:28
  19.8 3.3 %shard_map.129 = (bf16[1,128,2048]{2,1,0:T(8,128)(2,1)}, bf16[4,128,256]{2,1,0:T(8,128)(2,1)}) custom-call(s32[9]{0:T(128)} %pad_add_fusion.refs_0_, bf16[1,128,2048]{2,1,0:T(8,128)(2,1)} %refs_1_.7, bf16[1,128,2048]{2,1,0:T(8,128)(2,1)} %refs_2_.7, bf16[1,128,2048]{2,1,0:T(8,128)(2,1)} %refs_3_.6, f32[1,16,128]{2,1,0:T(8,128)} %refs_3_.7, ...), custom_call_target="tpu_custom_call" | custom-call | tf_op jit(solution)/shard_map/pallas_call | solution.py:194
  23.2 0.9 %add_convert_fusion.6.refs_1_ = bf16[4,128,128]{2,1,0:T(8,128)(2,1)S(1)} fusion(bf16[4,128,128]{2,1,0:T(8,128)(2,1)} %collective-permute-done.3, bf16[4,128,128]{2,1,0:T(8,128)(2,1)S(1)} %copy-done.8), kind=kLoop, calls=%fused_computation.18 | loop fusion | flops 262144 | bytes 393216 | tf_op jit(solution)/shard_map/convert_element_type | solution.py:240
  24.1 1.7 %collective-permute-start.7 = (bf16[4,128,128]{2,1,0:T(8,128)(2,1)S(1)}, bf16[4,128,128]{2,1,0:T(8,128)(2,1)S(1)}, u32[]{:S(2)}, u32[]{:S(2)}) collective-permute-start(bf16[4,128,128]{2,1,0:T(8,128)(2,1)S(1)} %add_convert_fusion.6.refs_1_), channel_id=1, source_target_pairs={{0,4},{2,6},{4,0},{6,2},{1,5},{3,7},{5,1},{7,3},{8,12},{10,14},{12... | collective-permute-start | bytes 393224 | tf_op jit(solution)/shard_map/ppermute | solution.py:28
  25.9 0.9 %add_convert_fusion.4.refs_1_ = bf16[4,128,128]{2,1,0:T(8,128)(2,1)S(1)} fusion(bf16[4,128,128]{2,1,0:T(8,128)(2,1)} %collective-permute-done.15, bf16[4,128,128]{2,1,0:T(8,128)(2,1)S(1)} %copy-done.7), kind=kLoop, calls=%fused_computation.16 | loop fusion | flops 262144 | bytes 393216 | tf_op jit(solution)/shard_map/convert_element_type | solution.py:240
  28.0 3.3 %shard_map.130 = (bf16[1,128,2048]{2,1,0:T(8,128)(2,1)}, bf16[4,128,256]{2,1,0:T(8,128)(2,1)}) custom-call(s32[9]{0:T(128)} %pad_add_fusion.refs_0_, bf16[1,128,2048]{2,1,0:T(8,128)(2,1)} %refs_1_.7, bf16[1,128,2048]{2,1,0:T(8,128)(2,1)} %refs_2_.7, bf16[1,128,2048]{2,1,0:T(8,128)(2,1)} %refs_3_.6, ...), custom_call_target="tpu_custom_call", output_to_operand_aliasing={{0}: (13, {}), {1}: (14, {})} | custom-call | tf_op jit(solution)/shard_map/pallas_call | solution.py:194
  31.3 1.0 %collective-permute-done.10.refs_4_ = bf16[128,1024]{1,0:T(8,128)(2,1)} collective-permute-done((bf16[128,1024]{1,0:T(8,128)(2,1)}, bf16[128,1024]{1,0:T(8,128)(2,1)}, u32[]{:S(2)}, u32[]{:S(2)}) %collective-permute-start.10) | collective-permute-done | bytes 262176 | tf_op jit(solution)/shard_map/ppermute | solution.py:28
  32.3 2.5 %turn.1.refs_3_ = bf16[1024,512]{1,0:T(8,128)(2,1)} custom-call(s32[9]{0:T(128)} %pad_add_fusion.refs_0_, bf16[128,1024]{1,0:T(8,128)(2,1)} %pad_maximum_fusion.refs_1_, bf16[128,1024]{1,0:T(8,128)(2,1)} %copy-done.10, bf16[128,1024]{1,0:T(8,128)(2,1)} %copy-done.11, bf16[128,1024]{1,0:T(8,128)(2,1)} %collective-permute-done.10.refs_4_), custom_call_target="tpu_custom_call" | custom-call | tf_op jit(solution)/shard_map/turn/pallas_call | solution.py:248
  34.8 1.1 %collective-permute-done.7.refs_2_ = bf16[4,128,128]{2,1,0:T(8,128)(2,1)S(1)} collective-permute-done((bf16[4,128,128]{2,1,0:T(8,128)(2,1)S(1)}, bf16[4,128,128]{2,1,0:T(8,128)(2,1)S(1)}, u32[]{:S(2)}, u32[]{:S(2)}) %collective-permute-start.7) | collective-permute-done | bytes 131104 | tf_op jit(solution)/shard_map/ppermute | solution.py:28
  36.5 2.5 %shard_map.131 = (bf16[512,128]{1,0:T(8,128)(2,1)}, bf16[512,128]{1,0:T(8,128)(2,1)}, bf16[128,128]{1,0:T(8,128)(2,1)}) custom-call(s32[9]{0:T(128)} %pad_add_fusion.refs_0_, bf16[4,128,128]{2,1,0:T(8,128)(2,1)} %copy-done.6, bf16[4,128,128]{2,1,0:T(8,128)(2,1)} %copy-done.15, bf16[1024,512]{1,0:T(8,128)(2,1)} %turn.1.refs_3_), custom_call_target="tpu_custom_call" | custom-call | tf_op jit(solution)/shard_map/pallas_call | solution.py:220
  39.0 1.7 %collective-permute-start.11 = (bf16[512,128]{1,0:T(8,128)(2,1)}, bf16[512,128]{1,0:T(8,128)(2,1)S(1)}, u32[]{:S(2)}, u32[]{:S(2)}) collective-permute-start(bf16[512,128]{1,0:T(8,128)(2,1)} %get-tuple-element.35), channel_id=1, source_target_pairs={{0,8},{8,0},{16,24},{24,16},{1,9},{9,1},{17,25},{25,17},{2,10},{10... | collective-permute-start | bytes 393224 | tf_op jit(solution)/shard_map/ppermute | solution.py:28
  41.4 2.5 %shard_map.133 = (bf16[512,128]{1,0:T(8,128)(2,1)}, bf16[512,128]{1,0:T(8,128)(2,1)}, bf16[128,128]{1,0:T(8,128)(2,1)}) custom-call(s32[9]{0:T(128)} %pad_add_fusion.refs_0_, bf16[4,128,128]{2,1,0:T(8,128)(2,1)} %copy-done.5, bf16[4,128,128]{2,1,0:T(8,128)(2,1)} %copy-done.14, bf16[1024,512]{1,0:T(8,128)(2,1)} %turn.1.refs_3_), custom_call_target="tpu_custom_call" | custom-call | tf_op jit(solution)/shard_map/pallas_call | solution.py:220
  43.9 0.8 %constant_dynamic-update-slice_fusion.1 = bf16[128,256]{1,0:T(8,128)(2,1)S(1)} fusion(bf16[128,128]{1,0:T(8,128)(2,1)} %get-tuple-element.39), kind=kLoop, calls=%fused_computation.37 | loop fusion | bytes 65536
  45.0 0.8 %constant_dynamic-update-slice_fusion = bf16[128,256]{1,0:T(8,128)(2,1)S(1)} fusion(bf16[128,256]{1,0:T(8,128)(2,1)S(1)} %constant_dynamic-update-slice_fusion.1, bf16[128,128]{1,0:T(8,128)(2,1)} %get-tuple-element.40), kind=kLoop, calls=%fused_computation.36 | loop fusion | bytes 65536 | tf_op jit(solution)/shard_map/concatenate | solution.py:262
  45.8 1.0 %add_convert_fusion.5 = bf16[512,128]{1,0:T(8,128)(2,1)S(1)} fusion(bf16[512,128]{1,0:T(8,128)(2,1)S(1)} %collective-permute-done.11, bf16[512,128]{1,0:T(8,128)(2,1)} %get-tuple-element.34), kind=kLoop, calls=%fused_computation.17 | loop fusion | flops 262144 | bytes 393216 | tf_op jit(solution)/shard_map/convert_element_type | solution.py:269
  46.8 2.8 %collective-permute-start.21 = (bf16[512,128]{1,0:T(8,128)(2,1)S(1)}, bf16[512,128]{1,0:T(8,128)(2,1)S(1)}, u32[]{:S(2)}, u32[]{:S(2)}) collective-permute-start(bf16[512,128]{1,0:T(8,128)(2,1)S(1)} %add_convert_fusion.5), channel_id=1, source_target_pairs={{0,16},{8,24},{16,0},{24,8},{1,17},{9,25},{17,1},{25,9},{2,18},{10... | collective-permute-start | bytes 393224 | tf_op jit(solution)/shard_map/ppermute | solution.py:28
  49.6 1.6 %collective-permute-start.13 = (bf16[128,256]{1,0:T(8,128)(2,1)S(1)}, bf16[128,256]{1,0:T(8,128)(2,1)S(1)}, u32[]{:S(2)}, u32[]{:S(2)}) collective-permute-start(bf16[128,256]{1,0:T(8,128)(2,1)S(1)} %get-tuple-element.55), channel_id=1, source_target_pairs={{0,4},{2,6},{4,0},{6,2},{1,5},{3,7},{5,1},{7,3},{8,12},{10,14},{12... | collective-permute-start | bytes 196616 | tf_op jit(solution)/shard_map/ppermute | solution.py:28
  51.5 0.9 %add_convert_fusion.3 = bf16[512,128]{1,0:T(8,128)(2,1)S(1)} fusion(bf16[512,128]{1,0:T(8,128)(2,1)S(1)} %collective-permute-done.17, bf16[512,128]{1,0:T(8,128)(2,1)} %get-tuple-element.41), kind=kLoop, calls=%fused_computation.15 | loop fusion | flops 262144 | bytes 393216 | tf_op jit(solution)/shard_map/convert_element_type | solution.py:269
  52.4 2.4 %collective-permute-start.19 = (bf16[512,128]{1,0:T(8,128)(2,1)S(1)}, bf16[512,128]{1,0:T(8,128)(2,1)S(1)}, u32[]{:S(2)}, u32[]{:S(2)}) collective-permute-start(bf16[512,128]{1,0:T(8,128)(2,1)S(1)} %add_convert_fusion.3), channel_id=1, source_target_pairs={{0,16},{8,24},{16,0},{24,8},{1,17},{9,25},{17,1},{25,9},{2,18},{10... | collective-permute-start | bytes 393224 | tf_op jit(solution)/shard_map/ppermute | solution.py:28
  55.3 1.6 %collective-permute-start.18 = (bf16[128,2048]{1,0:T(8,128)(2,1)S(1)}, bf16[128,2048]{1,0:T(8,128)(2,1)S(1)}, u32[]{:S(2)}, u32[]{:S(2)}) collective-permute-start(bf16[128,2048]{1,0:T(8,128)(2,1)S(1)} %convolution_convert_fusion), channel_id=1, source_target_pairs={{0,1},{1,0},{2,3},{3,2},{4,5},{5,4},{6,7},{7,6},{8,9},{9,8},{10,11... | collective-permute-start | bytes 1572872 | tf_op jit(solution)/shard_map/ppermute | solution.py:28
  57.5 4.3 %collective-permute-done.19 = bf16[512,128]{1,0:T(8,128)(2,1)S(1)} collective-permute-done((bf16[512,128]{1,0:T(8,128)(2,1)S(1)}, bf16[512,128]{1,0:T(8,128)(2,1)S(1)}, u32[]{:S(2)}, u32[]{:S(2)}) %collective-permute-start.19) | collective-permute-done | bytes 131104 | tf_op jit(solution)/shard_map/ppermute | solution.py:28
  62.0 2.1 %collective-permute-start.22 = (bf16[512,128]{1,0:T(8,128)(2,1)S(1)}, bf16[512,128]{1,0:T(8,128)(2,1)S(1)}, u32[]{:S(2)}, u32[]{:S(2)}) collective-permute-start(bf16[512,128]{1,0:T(8,128)(2,1)S(1)} %add_convert_fusion.1), channel_id=1, source_target_pairs={{0,8},{8,0},{16,24},{24,16},{1,9},{9,1},{17,25},{25,17},{2,10},{10... | collective-permute-start | bytes 393224 | tf_op jit(solution)/shard_map/ppermute | solution.py:28
  64.1 4.1 %collective-permute-done.20 = bf16[512,128]{1,0:T(8,128)(2,1)S(1)} collective-permute-done((bf16[512,128]{1,0:T(8,128)(2,1)S(1)}, bf16[512,128]{1,0:T(8,128)(2,1)S(1)}, u32[]{:S(2)}, u32[]{:S(2)}) %collective-permute-start.20) | collective-permute-done | bytes 131104 | tf_op jit(solution)/shard_map/ppermute | solution.py:28
  68.2 1.3 %fusion.5 = bf16[1,128,2048]{2,1,0:T(8,128)(2,1)} fusion(bf16[128,2048]{1,0:T(8,128)(2,1)S(1)} %collective-permute-done.18, bf16[128,256]{1,0:T(8,128)(2,1)S(1)} %constant_dynamic-update-slice_fusion, bf16[4096,256]{1,0:T(8,128)(2,1)S(1)} %copy-done, s32[]{:T(128)S(6)} %select_n.58), kind=kOutput, calls=%fused_computation.6 | convolution fusion | flops 135004160 | bytes 2162692 | tf_op jit(solution)/shard_map/te,de->td/dot_general | solution.py:285
  69.6 1.1 %convert_multiply_fusion = f32[1024,256]{1,0:T(8,128)} fusion(bf16[1024,128]{1,0:T(8,128)(2,1)S(1)} %maximum_select_fusion.1, bf16[1024,128]{1,0:T(8,128)(2,1)S(1)} %maximum_select_fusion), kind=kLoop, calls=%fused_computation.1 | loop fusion | flops 1310720 | bytes 1572864 | tf_op jit(solution)/shard_map/mul | solution.py:317
  (76 shorter events, 9.4 us)
Async XLA Ops:
  0.6 54.2 %copy-start = (bf16[4096,256]{1,0:T(8,128)(2,1)S(1)}, bf16[4096,256]{1,0:T(8,128)(2,1)}, u32[]{:S(2)}) copy-start(bf16[4096,256]{1,0:T(8,128)(2,1)} %param.17) | copy-start | bytes 6291460
  0.6 8.0 %copy-start.12 = (bf16[1,128,256]{2,1,0:T(8,128)(2,1)S(1)}, bf16[1,128,256]{2,1,0:T(8,128)(2,1)}, u32[]{:S(2)}) copy-start(bf16[1,128,256]{2,1,0:T(8,128)(2,1)} %refs_9_.3) | copy-start | bytes 196612
  0.7 7.4 %copy-start.16 = (s32[8]{0:T(128)S(1)}, s32[8]{0:T(128)}, u32[]{:S(2)}) copy-start(s32[8]{0:T(128)} %param.16) | copy-start | bytes 100
  0.7 8.0 %collective-permute-start = (bf16[1,128,256]{2,1,0:T(8,128)(2,1)}, bf16[1,128,256]{2,1,0:T(8,128)(2,1)S(1)}, u32[]{:S(2)}, u32[]{:S(2)}) collective-permute-start(bf16[1,128,256]{2,1,0:T(8,128)(2,1)} %refs_4_.7), channel_id=1, source_target_pairs={{0,2},{2,0},{4,6},{6,4},{1,3},{3,1},{5,7},{7,5},{8,10},{10,8},{12,... | collective-permute-start | bytes 196616 | tf_op jit(solution)/shard_map/ppermute | solution.py:28
  1.2 7.5 %collective-permute-start.1 = (bf16[1,128,256]{2,1,0:T(8,128)(2,1)}, bf16[1,128,256]{2,1,0:T(8,128)(2,1)S(1)}, u32[]{:S(2)}, u32[]{:S(2)}) collective-permute-start(bf16[1,128,256]{2,1,0:T(8,128)(2,1)} %refs_4_.7), channel_id=1, source_target_pairs={{0,4},{2,6},{4,0},{6,2},{1,5},{3,7},{5,1},{7,3},{8,12},{10,14},{12... | collective-permute-start | bytes 196616 | tf_op jit(solution)/shard_map/ppermute | solution.py:28
  3.8 5.0 %collective-permute-start.2 = (bf16[1,128,256]{2,1,0:T(8,128)(2,1)}, bf16[1,128,256]{2,1,0:T(8,128)(2,1)S(1)}, u32[]{:S(2)}, u32[]{:S(2)}) collective-permute-start(bf16[1,128,256]{2,1,0:T(8,128)(2,1)} %refs_4_.7), channel_id=1, source_target_pairs={{0,6},{2,4},{4,2},{6,0},{1,7},{3,5},{5,3},{7,1},{8,14},{10,12},{12... | collective-permute-start | bytes 196616 | tf_op jit(solution)/shard_map/ppermute | solution.py:28
  3.8 13.6 %collective-permute-start.4 = (bf16[1,128,256]{2,1,0:T(8,128)(2,1)}, bf16[1,128,256]{2,1,0:T(8,128)(2,1)S(1)}, u32[]{:S(2)}, u32[]{:S(2)}) collective-permute-start(bf16[1,128,256]{2,1,0:T(8,128)(2,1)} %refs_9_.3), channel_id=1, source_target_pairs={{0,2},{2,0},{4,6},{6,4},{1,3},{3,1},{5,7},{7,5},{8,10},{10,8},{12,... | collective-permute-start | bytes 196616 | tf_op jit(solution)/shard_map/ppermute | solution.py:28
  4.0 14.0 %collective-permute-start.5 = (bf16[1,128,256]{2,1,0:T(8,128)(2,1)}, bf16[1,128,256]{2,1,0:T(8,128)(2,1)}, u32[]{:S(2)}, u32[]{:S(2)}) collective-permute-start(bf16[1,128,256]{2,1,0:T(8,128)(2,1)} %refs_9_.3), channel_id=1, source_target_pairs={{0,4},{2,6},{4,0},{6,2},{1,5},{3,7},{5,1},{7,3},{8,12},{10,14},{12... | collective-permute-start | bytes 196616 | tf_op jit(solution)/shard_map/ppermute | solution.py:28
  8.7 11.0 %collective-permute-start.6 = (bf16[1,128,256]{2,1,0:T(8,128)(2,1)S(1)}, bf16[1,128,256]{2,1,0:T(8,128)(2,1)}, u32[]{:S(2)}, u32[]{:S(2)}) collective-permute-start(bf16[1,128,256]{2,1,0:T(8,128)(2,1)S(1)} %copy-done.12), channel_id=1, source_target_pairs={{0,6},{2,4},{4,2},{6,0},{1,7},{3,5},{5,3},{7,1},{8,14},{10,12},{12... | collective-permute-start | bytes 196616 | tf_op jit(solution)/shard_map/ppermute | solution.py:28
  12.7 10.4 %collective-permute-start.15 = (bf16[4,128,128]{2,1,0:T(8,128)(2,1)}, bf16[4,128,128]{2,1,0:T(8,128)(2,1)}, u32[]{:S(2)}, u32[]{:S(2)}) collective-permute-start(bf16[4,128,128]{2,1,0:T(8,128)(2,1)} %shard_map.132), channel_id=1, source_target_pairs={{0,2},{2,0},{4,6},{6,4},{1,3},{3,1},{5,7},{7,5},{8,10},{10,8},{12,... | collective-permute-start | bytes 393224 | tf_op jit(solution)/shard_map/ppermute | solution.py:28
  15.6 7.6 %copy-start.8 = (bf16[4,128,128]{2,1,0:T(8,128)(2,1)S(1)}, bf16[4,128,128]{2,1,0:T(8,128)(2,1)}, u32[]{:S(2)}) copy-start(bf16[4,128,128]{2,1,0:T(8,128)(2,1)} %shard_map.128) | copy-start | bytes 393220
  15.6 10.3 %copy-start.7 = (bf16[4,128,128]{2,1,0:T(8,128)(2,1)S(1)}, bf16[4,128,128]{2,1,0:T(8,128)(2,1)}, u32[]{:S(2)}) copy-start(bf16[4,128,128]{2,1,0:T(8,128)(2,1)} %shard_map.132) | copy-start | bytes 393220
  15.6 7.6 %collective-permute-start.3 = (bf16[4,128,128]{2,1,0:T(8,128)(2,1)}, bf16[4,128,128]{2,1,0:T(8,128)(2,1)}, u32[]{:S(2)}, u32[]{:S(2)}) collective-permute-start(bf16[4,128,128]{2,1,0:T(8,128)(2,1)} %shard_map.128), channel_id=1, source_target_pairs={{0,2},{2,0},{4,6},{6,4},{1,3},{3,1},{5,7},{7,5},{8,10},{10,8},{12,... | collective-permute-start | bytes 393224 | tf_op jit(solution)/shard_map/ppermute | solution.py:28
  17.4 13.9 %collective-permute-start.8 = (bf16[128,1024]{1,0:T(8,128)(2,1)}, bf16[128,1024]{1,0:T(8,128)(2,1)S(1)}, u32[]{:S(2)}, u32[]{:S(2)}) collective-permute-start(bf16[128,1024]{1,0:T(8,128)(2,1)} %pad_maximum_fusion.1), channel_id=1, source_target_pairs={{0,2},{2,0},{4,6},{6,4},{1,3},{3,1},{5,7},{7,5},{8,10},{10,8},{12,... | collective-permute-start | bytes 786440 | tf_op jit(solution)/shard_map/ppermute | solution.py:28
  18.1 13.3 %collective-permute-start.9 = (bf16[128,1024]{1,0:T(8,128)(2,1)}, bf16[128,1024]{1,0:T(8,128)(2,1)S(1)}, u32[]{:S(2)}, u32[]{:S(2)}) collective-permute-start(bf16[128,1024]{1,0:T(8,128)(2,1)} %pad_maximum_fusion.2), channel_id=1, source_target_pairs={{0,4},{2,6},{4,0},{6,2},{1,5},{3,7},{5,1},{7,3},{8,12},{10,14},{12... | collective-permute-start | bytes 786440 | tf_op jit(solution)/shard_map/ppermute | solution.py:28
  19.7 12.6 %collective-permute-start.10 = (bf16[128,1024]{1,0:T(8,128)(2,1)}, bf16[128,1024]{1,0:T(8,128)(2,1)}, u32[]{:S(2)}, u32[]{:S(2)}) collective-permute-start(bf16[128,1024]{1,0:T(8,128)(2,1)} %pad_maximum_fusion.3), channel_id=1, source_target_pairs={{0,6},{2,4},{4,2},{6,0},{1,7},{3,5},{5,3},{7,1},{8,14},{10,12},{12... | collective-permute-start | bytes 786440 | tf_op jit(solution)/shard_map/ppermute | solution.py:28
  24.1 10.7 %copy-start.6 = (bf16[4,128,128]{2,1,0:T(8,128)(2,1)}, bf16[4,128,128]{2,1,0:T(8,128)(2,1)S(1)}, u32[]{:S(2)}) copy-start(bf16[4,128,128]{2,1,0:T(8,128)(2,1)S(1)} %add_convert_fusion.6.refs_1_) | copy-start | bytes 393220
  24.1 11.7 %collective-permute-start.7 = (bf16[4,128,128]{2,1,0:T(8,128)(2,1)S(1)}, bf16[4,128,128]{2,1,0:T(8,128)(2,1)S(1)}, u32[]{:S(2)}, u32[]{:S(2)}) collective-permute-start(bf16[4,128,128]{2,1,0:T(8,128)(2,1)S(1)} %add_convert_fusion.6.refs_1_), channel_id=1, source_target_pairs={{0,4},{2,6},{4,0},{6,2},{1,5},{3,7},{5,1},{7,3},{8,12},{10,14},{12... | collective-permute-start | bytes 393224 | tf_op jit(solution)/shard_map/ppermute | solution.py:28
  26.8 8.0 %copy-start.5 = (bf16[4,128,128]{2,1,0:T(8,128)(2,1)}, bf16[4,128,128]{2,1,0:T(8,128)(2,1)S(1)}, u32[]{:S(2)}) copy-start(bf16[4,128,128]{2,1,0:T(8,128)(2,1)S(1)} %add_convert_fusion.4.refs_1_) | copy-start | bytes 393220
  26.8 13.9 %collective-permute-start.16 = (bf16[4,128,128]{2,1,0:T(8,128)(2,1)S(1)}, bf16[4,128,128]{2,1,0:T(8,128)(2,1)S(1)}, u32[]{:S(2)}, u32[]{:S(2)}) collective-permute-start(bf16[4,128,128]{2,1,0:T(8,128)(2,1)S(1)} %add_convert_fusion.4.refs_1_), channel_id=1, source_target_pairs={{0,4},{2,6},{4,0},{6,2},{1,5},{3,7},{5,1},{7,3},{8,12},{10,14},{12... | collective-permute-start | bytes 393224 | tf_op jit(solution)/shard_map/ppermute | solution.py:28
  34.8 14.7 %copy-start.1 = (bf16[4,128,256]{2,1,0:T(8,128)(2,1)S(1)}, bf16[4,128,256]{2,1,0:T(8,128)(2,1)}, u32[]{:S(2)}) copy-start(bf16[4,128,256]{2,1,0:T(8,128)(2,1)} %get-tuple-element.36) | copy-start | bytes 786436
  39.0 6.7 %collective-permute-start.11 = (bf16[512,128]{1,0:T(8,128)(2,1)}, bf16[512,128]{1,0:T(8,128)(2,1)S(1)}, u32[]{:S(2)}, u32[]{:S(2)}) collective-permute-start(bf16[512,128]{1,0:T(8,128)(2,1)} %get-tuple-element.35), channel_id=1, source_target_pairs={{0,8},{8,0},{16,24},{24,16},{1,9},{9,1},{17,25},{25,17},{2,10},{10... | collective-permute-start | bytes 393224 | tf_op jit(solution)/shard_map/ppermute | solution.py:28
  44.7 6.8 %collective-permute-start.17 = (bf16[512,128]{1,0:T(8,128)(2,1)}, bf16[512,128]{1,0:T(8,128)(2,1)S(1)}, u32[]{:S(2)}, u32[]{:S(2)}) collective-permute-start(bf16[512,128]{1,0:T(8,128)(2,1)} %get-tuple-element.42), channel_id=1, source_target_pairs={{0,8},{8,0},{16,24},{24,16},{1,9},{9,1},{17,25},{25,17},{2,10},{10... | collective-permute-start | bytes 393224 | tf_op jit(solution)/shard_map/ppermute | solution.py:28
  45.8 22.5 %copy-start.9 = (bf16[128,256]{1,0:T(8,128)(2,1)}, bf16[128,256]{1,0:T(8,128)(2,1)S(1)}, u32[]{:S(2)}) copy-start(bf16[128,256]{1,0:T(8,128)(2,1)S(1)} %constant_dynamic-update-slice_fusion) | copy-start | bytes 196612
  46.8 15.2 %collective-permute-start.21 = (bf16[512,128]{1,0:T(8,128)(2,1)S(1)}, bf16[512,128]{1,0:T(8,128)(2,1)S(1)}, u32[]{:S(2)}, u32[]{:S(2)}) collective-permute-start(bf16[512,128]{1,0:T(8,128)(2,1)S(1)} %add_convert_fusion.5), channel_id=1, source_target_pairs={{0,16},{8,24},{16,0},{24,8},{1,17},{9,25},{17,1},{25,9},{2,18},{10... | collective-permute-start | bytes 393224 | tf_op jit(solution)/shard_map/ppermute | solution.py:28
  49.5 5.7 %collective-permute-start.14 = (bf16[128,256]{1,0:T(8,128)(2,1)S(1)}, bf16[128,256]{1,0:T(8,128)(2,1)S(1)}, u32[]{:S(2)}, u32[]{:S(2)}) collective-permute-start(bf16[128,256]{1,0:T(8,128)(2,1)S(1)} %get-tuple-element.54), channel_id=1, source_target_pairs={{0,6},{2,4},{4,2},{6,0},{1,7},{3,5},{5,3},{7,1},{8,14},{10,12},{12... | collective-permute-start | bytes 196616 | tf_op jit(solution)/shard_map/ppermute | solution.py:28
  49.6 7.2 %collective-permute-start.13 = (bf16[128,256]{1,0:T(8,128)(2,1)S(1)}, bf16[128,256]{1,0:T(8,128)(2,1)S(1)}, u32[]{:S(2)}, u32[]{:S(2)}) collective-permute-start(bf16[128,256]{1,0:T(8,128)(2,1)S(1)} %get-tuple-element.55), channel_id=1, source_target_pairs={{0,4},{2,6},{4,0},{6,2},{1,5},{3,7},{5,1},{7,3},{8,12},{10,14},{12... | collective-permute-start | bytes 196616 | tf_op jit(solution)/shard_map/ppermute | solution.py:28
  51.2 5.6 %collective-permute-start.12 = (bf16[128,256]{1,0:T(8,128)(2,1)S(1)}, bf16[128,256]{1,0:T(8,128)(2,1)S(1)}, u32[]{:S(2)}, u32[]{:S(2)}) collective-permute-start(bf16[128,256]{1,0:T(8,128)(2,1)S(1)} %get-tuple-element.53), channel_id=1, source_target_pairs={{0,2},{2,0},{4,6},{6,4},{1,3},{3,1},{5,7},{7,5},{8,10},{10,8},{12,... | collective-permute-start | bytes 196616 | tf_op jit(solution)/shard_map/ppermute | solution.py:28
  52.4 9.4 %collective-permute-start.19 = (bf16[512,128]{1,0:T(8,128)(2,1)S(1)}, bf16[512,128]{1,0:T(8,128)(2,1)S(1)}, u32[]{:S(2)}, u32[]{:S(2)}) collective-permute-start(bf16[512,128]{1,0:T(8,128)(2,1)S(1)} %add_convert_fusion.3), channel_id=1, source_target_pairs={{0,16},{8,24},{16,0},{24,8},{1,17},{9,25},{17,1},{25,9},{2,18},{10... | collective-permute-start | bytes 393224 | tf_op jit(solution)/shard_map/ppermute | solution.py:28
  55.3 12.9 %collective-permute-start.18 = (bf16[128,2048]{1,0:T(8,128)(2,1)S(1)}, bf16[128,2048]{1,0:T(8,128)(2,1)S(1)}, u32[]{:S(2)}, u32[]{:S(2)}) collective-permute-start(bf16[128,2048]{1,0:T(8,128)(2,1)S(1)} %convolution_convert_fusion), channel_id=1, source_target_pairs={{0,1},{1,0},{2,3},{3,2},{4,5},{5,4},{6,7},{7,6},{8,9},{9,8},{10,11... | collective-permute-start | bytes 1572872 | tf_op jit(solution)/shard_map/ppermute | solution.py:28
  61.9 6.3 %collective-permute-start.20 = (bf16[512,128]{1,0:T(8,128)(2,1)S(1)}, bf16[512,128]{1,0:T(8,128)(2,1)S(1)}, u32[]{:S(2)}, u32[]{:S(2)}) collective-permute-start(bf16[512,128]{1,0:T(8,128)(2,1)S(1)} %add_convert_fusion.2), channel_id=1, source_target_pairs={{0,8},{8,0},{16,24},{24,16},{1,9},{9,1},{17,25},{25,17},{2,10},{10... | collective-permute-start | bytes 393224 | tf_op jit(solution)/shard_map/ppermute | solution.py:28
  62.0 7.5 %collective-permute-start.22 = (bf16[512,128]{1,0:T(8,128)(2,1)S(1)}, bf16[512,128]{1,0:T(8,128)(2,1)S(1)}, u32[]{:S(2)}, u32[]{:S(2)}) collective-permute-start(bf16[512,128]{1,0:T(8,128)(2,1)S(1)} %add_convert_fusion.1), channel_id=1, source_target_pairs={{0,8},{8,0},{16,24},{24,16},{1,9},{9,1},{17,25},{25,17},{2,10},{10... | collective-permute-start | bytes 393224 | tf_op jit(solution)/shard_map/ppermute | solution.py:28
  (8 other events, 5.8 us)
